TPU v7x, 512 devices: a whole 4x8x8 slice. The times are simulated.
512 devices in a mesh: dp: 16 (over y_lo, x), space: 32 (over z, y_hi, core).
Axes of the slice: x: 4, y: 8 (y_hi: 2, y_lo: 4; y = y_hi * 4 + y_lo), z: 8, core: 2. Of those that a mesh axis runs over, the one named last changes fastest.
Arguments:
- fields: bfloat16 [16, 100, 131072], P('dp', None, 'space'), may hold values from -6 to 6
- cell_index: int32 [1024, 128], P('space'), may hold values from 0 to 6143
- interp_weight: bfloat16 [1024, 16, 128], P('space'), may hold values from 0 to 2, as said below
- w_in: bfloat16 [100, 1024], replicated, may hold values from -0.625 to 0.625
- ln_gain: float32 [1024], replicated, may hold values from 0.5 to 1.5
- w_qkv: bfloat16 [1024, 3072], P('dp'), may hold values from -0.1875 to 0.1875
- w_out: bfloat16 [1024, 1024], P('dp'), may hold values from -3 to 3
Outputs:
- latent: bfloat16 [16, 16384, 1024], P('dp', 'space')
- update: bfloat16 [16, 16384, 1024], P('dp', 'space')
Inputs may be any that keep to these rules, and one draw needn't show every extreme that they name: `interp_weight`: in each block the slots from some count on carry zero weight for all its 16 nodes; that count lies between 48 and 128. `cell_index`: indexes a shard's 4096 cells extended by 1024 cells of each neighbouring shard, lower neighbour first.
All inputs are finite; a program needn't handle non-finite values.
Results may differ from a plain program's by a relative error of at most 0.0068.
Values may be sent and summed in bfloat16 or wider, within the bound.
A program may use at most 128 MiB of HBM per device.

v0:
```python
import math
import jax
import jax.numpy as jnp
from jax import lax
from jax.sharding import PartitionSpec as P

HEADS = 16


def padded(array, sides, width):
    for axis, dim in sides:
        size, length = (lax.axis_size(axis), array.shape[dim])
        up = [(i, (i + 1) % size) for i in range(size)]
        down = [(j, i) for i, j in up]
        last = lax.slice_in_dim(array, length - width, length, axis=dim)
        first = lax.slice_in_dim(array, 0, width, axis=dim)
        before = lax.ppermute(last, axis, up)
        after = lax.ppermute(first, axis, down)
        array = jnp.concatenate([before, array, after], axis=dim)
    return array


def unit_heads(projected):
    head_size = projected.shape[1] // HEADS
    head_rows = projected.reshape(projected.shape[0], HEADS, head_size)
    scale_rows = jnp.sqrt(jnp.mean(head_rows * head_rows, axis=-1, keepdims=True) + 1e-06)
    return (head_rows / scale_rows).astype(jnp.bfloat16).reshape(projected.shape)


def shards(fields, cell_index, interp_weight, w_in, ln_gain, w_qkv, w_out):
    width = w_qkv.shape[1] // 3
    full_qkv, full_out = (
        lax.all_gather(w_qkv, "dp", axis=0, tiled=True),
        lax.all_gather(w_out, "dp", axis=0, tiled=True),
    )
    grid_field = fields[0]
    cell_count = grid_field.shape[1]
    cell_reach = cell_count // 4
    extended = padded(grid_field, (("space", 1),), cell_reach)
    picked = jnp.take(extended, cell_index, axis=1)
    encoded = jnp.einsum("cbs,bns->bnc", picked, interp_weight, preferred_element_type=jnp.float32)
    node_count = encoded.shape[0] * encoded.shape[1]
    encoded = encoded.reshape(node_count, encoded.shape[2]).astype(jnp.bfloat16)
    embedded = jnp.dot(encoded, w_in, preferred_element_type=jnp.float32)
    average = jnp.mean(embedded, axis=1, keepdims=True)
    centered = embedded - average
    spread = jnp.mean(centered * centered, axis=1, keepdims=True)
    normed = (centered / jnp.sqrt(spread + 1e-05) * ln_gain).astype(jnp.bfloat16)
    margin = node_count // 2
    bordered = padded(normed, (("space", 0),), margin)
    side_normed = jnp.concatenate([bordered[:margin], bordered[margin + node_count :]], axis=0)
    projected = jnp.dot(normed, full_qkv, preferred_element_type=jnp.float32)
    side_projected = jnp.dot(side_normed, full_qkv[:, width:], preferred_element_type=jnp.float32)
    queries = unit_heads(projected[:, :width])
    own_pairs = jnp.concatenate(
        [
            unit_heads(projected[:, width : 2 * width]),
            projected[:, 2 * width :].astype(jnp.bfloat16),
        ],
        axis=1,
    )
    side_pairs = jnp.concatenate(
        [unit_heads(side_projected[:, :width]), side_projected[:, width:].astype(jnp.bfloat16)],
        axis=1,
    )
    window = jnp.concatenate([side_pairs[:margin], own_pairs, side_pairs[margin:]], axis=0)
    head_size = width // HEADS
    group_width = 2 * head_size

    def attend(group_index):
        offset = group_index * group_width
        query_group = lax.dynamic_slice_in_dim(queries, offset, group_width, 1).reshape(
            node_count, 2, head_size
        )
        key_group = lax.dynamic_slice_in_dim(window, offset, group_width, 1).reshape(
            window.shape[0], 2, head_size
        )
        value_group = lax.dynamic_slice_in_dim(window, width + offset, group_width, 1).reshape(
            window.shape[0], 2, head_size
        )
        scores = jnp.einsum(
            "qhd,khd->hqk", query_group, key_group, preferred_element_type=jnp.float32
        ) / math.sqrt(head_size)
        weights = jnp.exp(scores)
        probs = (weights / jnp.sum(weights, axis=2, keepdims=True)).astype(jnp.bfloat16)
        mixed_rows = jnp.einsum(
            "hqk,khd->qhd", probs, value_group, preferred_element_type=jnp.float32
        )
        return mixed_rows.astype(jnp.bfloat16).reshape(node_count, group_width)

    grouped = lax.map(attend, jnp.arange(HEADS // 2, dtype=jnp.int32))
    attended = grouped.transpose(1, 0, 2).reshape(node_count, width)
    update = jnp.dot(attended, full_out, preferred_element_type=jnp.float32)
    return (embedded.astype(jnp.bfloat16)[None], update.astype(jnp.bfloat16)[None])


def solution(mesh):
    placed = (
        P("dp", None, "space"),
        P("space", None),
        P("space", None, None),
        P(),
        P(),
        P("dp", None),
        P("dp", None),
    )
    return jax.shard_map(
        shards,
        mesh=mesh,
        in_specs=placed,
        out_specs=(P("dp", "space", None), P("dp", "space", None)),
        check_vma=False,
    )
```

profile of v0, /device:TPU:256, one launch (start us, length us, event | category | flops | bytes accessed | tf_op | source)
XLA Modules:
  0.0 250.1 jit_solution(16279916706704496909)
XLA Ops:
  9.6 6.3 %collective-permute-start.1 = (bf16[100,1024]{0,1:T(8,128)(2,1)S(1)}, bf16[100,1024]{0,1:T(8,128)(2,1)S(1)}, u32[]{:S(2)}, u32[]{:S(2)}) collective-permute-start(bf16[100,1024]{0,1:T(8,128)(2,1)S(1)} %get-tuple-element.101), channel_id=1, source_target_pairs={{1,0},{2,1},{3,2},{4,3},{5,4},{6,5},{7,6},{8,7},{9,8},{10,9},{11,1... | collective-permute-start | bytes 614408 | tf_op jit(solution)/shard_map/ppermute | solution.py:18
  15.9 1.9 collective-permute-start
  17.9 2.6 %collective-permute-done.1 = bf16[100,1024]{0,1:T(8,128)(2,1)S(1)} collective-permute-done((bf16[100,1024]{0,1:T(8,128)(2,1)S(1)}, bf16[100,1024]{0,1:T(8,128)(2,1)S(1)}, u32[]{:S(2)}, u32[]{:S(2)}) %collective-permute-start.1) | collective-permute-done | bytes 204832 | tf_op jit(solution)/shard_map/ppermute | solution.py:18
  20.4 12.3 %collective-permute-done = bf16[100,1024]{0,1:T(8,128)(2,1)S(1)} collective-permute-done((bf16[100,1024]{0,1:T(8,128)(2,1)S(1)}, bf16[100,1024]{0,1:T(8,128)(2,1)S(1)}, u32[]{:S(2)}, u32[]{:S(2)}) %collective-permute-start) | collective-permute-done | bytes 204832 | tf_op jit(solution)/shard_map/ppermute | solution.py:17
  33.1 12.1 %gather_fusion = bf16[4096,100]{1,0:T(8,128)(2,1)S(1)} fusion(bf16[100,6144]{0,1:T(8,128)(2,1)S(1)} %pad_maximum_fusion, s32[4096]{0:T(1024)S(1)} %bitcast_clamp_fusion), kind=kCustom, calls=%fused_computation | custom fusion | bytes 1654784 | tf_op jit(solution)/shard_map/jit(_take)/gather | solution.py:40
  49.9 1.9 collective-permute-start.3
  51.8 2.6 %collective-permute-start.2 = (bf16[256,1024]{1,0:T(8,128)(2,1)S(1)}, bf16[256,1024]{1,0:T(8,128)(2,1)S(1)}, u32[]{:S(2)}, u32[]{:S(2)}) collective-permute-start(bf16[256,1024]{1,0:T(8,128)(2,1)S(1)} %get-tuple-element.98), channel_id=1, source_target_pairs={{0,1},{1,2},{2,3},{3,4},{4,5},{5,6},{6,7},{7,8},{8,9},{9,10},{10,1... | collective-permute-start | bytes 1572872 | tf_op jit(solution)/shard_map/ppermute | solution.py:17
  54.5 19.2 %collective-permute-done.3 = bf16[256,1024]{1,0:T(8,128)(2,1)S(1)} collective-permute-done((bf16[256,1024]{1,0:T(8,128)(2,1)S(1)}, bf16[256,1024]{1,0:T(8,128)(2,1)S(1)}, u32[]{:S(2)}, u32[]{:S(2)}) %collective-permute-start.3) | collective-permute-done | bytes 524320 | tf_op jit(solution)/shard_map/ppermute | solution.py:18
  73.7 8.8 %collective-permute-done.2 = bf16[256,1024]{1,0:T(8,128)(2,1)S(1)} collective-permute-done((bf16[256,1024]{1,0:T(8,128)(2,1)S(1)}, bf16[256,1024]{1,0:T(8,128)(2,1)S(1)}, u32[]{:S(2)}, u32[]{:S(2)}) %collective-permute-start.2) | collective-permute-done | bytes 524320 | tf_op jit(solution)/shard_map/ppermute | solution.py:17
  82.5 45.7 %all-gather.3.cloned.1.call-done = bf16[1024,3072]{1,0:T(8,128)(2,1)} async-done(((bf16[64,3072]{1,0:T(8,128)(2,1)}), bf16[1024,3072]{1,0:T(8,128)(2,1)}) %all-gather.3.cloned.1.call-update) | async-done | bytes 6291472 | tf_op jit(solution)/shard_map/all_gather | solution.py:33
  128.2 4.7 %fusion.8 = f32[512,2048]{1,0:T(8,128)S(1)} fusion(bf16[1024,3072]{1,0:T(8,128)(2,1)} %all-gather.3.cloned.1.call-done, bf16[256,1024]{1,0:T(8,128)(2,1)S(1)} %collective-permute-done.3, bf16[256,1024]{1,0:T(8,128)(2,1)S(1)} %collective-permute-done.2), kind=kOutput, calls=%fused_computation.16 | convolution fusion | flops 2149580800 | bytes 9437184 | tf_op jit(solution)/shard_map/dot_general | solution.py:53
  136.1 3.4 %fusion.24 = f32[512,3072]{1,0:T(8,128)S(1)} fusion(bf16[512,1024]{1,0:T(8,128)(2,1)S(1)} %copy-done.6, bf16[1024,3072]{1,0:T(8,128)(2,1)S(1)} %copy-done.10), kind=kOutput, calls=%fused_computation.59 | convolution fusion | flops 3221225472 | bytes 13631488 | tf_op jit(solution)/shard_map/dot_general | solution.py:52
  142.5 2.4 slice_multiply_fusion
  150.8 2.6 %divide_convert_fusion.6 = bf16[512,1024]{1,0:T(8,128)(2,1)S(1)} fusion(f32[512,1024]{1,0:T(8,128)} %copy.16, f32[512,2048]{1,0:T(8,128)} %copy-done.3), kind=kLoop, calls=%fused_computation.27 | loop fusion | flops 1048576 | bytes 5242880 | tf_op jit(solution)/shard_map/convert_element_type | solution.py:27
  153.4 2.9 %copy.19 = f32[512,1024]{0,1:T(8,128)} copy(f32[512,1024]{1,0:T(8,128)} %get-tuple-element.94) | data formatting | bytes 4194304 | tf_op jit(solution)/shard_map/mul | solution.py:26
  156.3 1.9 bitcast_reduce_fusion
  159.9 2.9 %copy.20 = f32[512,1024]{1,0:T(8,128)} copy(f32[512,1024]{0,1:T(8,128)} %bitcast.62) | data formatting | bytes 4194304 | tf_op jit(solution)/shard_map/div | solution.py:27
  162.8 2.9 %copy.17 = f32[512,1024]{0,1:T(8,128)} copy(f32[512,1024]{1,0:T(8,128)} %get-tuple-element.95) | data formatting | bytes 4194304 | tf_op jit(solution)/shard_map/mul | solution.py:26
  169.2 2.9 %copy.18 = f32[512,1024]{1,0:T(8,128)} copy(f32[512,1024]{0,1:T(8,128)} %bitcast.63) | data formatting | bytes 4194304 | tf_op jit(solution)/shard_map/div | solution.py:27
  172.1 4.3 %divide_convert_fusion.4 = (bf16[512,1024]{1,0:T(8,128)(2,1)S(1)}, bf16[512,1024]{1,0:T(8,128)(2,1)S(1)}) fusion(f32[512,1024]{1,0:T(8,128)} %copy.20, f32[512,3072]{1,0:T(8,128)} %copy-done.2, f32[512,1024]{1,0:T(8,128)} %copy.18), kind=kLoop, calls=%fused_computation.25 | loop fusion | flops 2097152 | bytes 10485760 | tf_op jit(solution)/shard_map/convert_element_type | solution.py:27
  177.7 20.1 %fusion.7 = bf16[1024,2048]{1,0:T(8,128)(2,1)} fusion(bf16[512,1024]{1,0:T(8,128)(2,1)S(1)} %slice.81, bf16[512,1024]{1,0:T(8,128)(2,1)S(1)} %divide_convert_fusion.6, bf16[512,1024]{1,0:T(8,128)(2,1)S(1)} %copy-done.4, bf16[512,1024]{1,0:T(8,128)(2,1)S(1)} %get-tuple-element.93, bf16[256,2048]{1,0:T(8,128)(2,1)S(1)} %fusion.11), kind=kLoop, calls=%fused_computation.15 | loop fusion | flops 27262976 | bytes 9437184 | tf_op jit(solution)/shard_map/concatenate | solution.py:66
  197.8 6.5 %copy.21 = bf16[1024,2048]{0,1:T(8,128)(2,1)} copy(bf16[1024,2048]{1,0:T(8,128)(2,1)} %fusion.7) | data formatting | bytes 8388608 | tf_op jit(solution)/shard_map/while | solution.py:91
  204.3 34.9 %while.12 = (s32[]{:T(128)}, bf16[8,512,128]{1,2,0:T(8,128)(2,1)S(1)}, s32[8]{0:T(128)S(1)}, bf16[1024,2048]{0,1:T(8,128)(2,1)}, bf16[512,1024]{1,0:T(8,128)(2,1...) while((s32[]{:T(128)}, ...), condition=%wide.region_7.8_spmd, body=%wide.region_5.7_spmd.sunk | while | flops 273742848 | bytes 11018490 | solution.py:91
  239.3 3.9 %fusion.10 = bf16[1,512,1024]{2,1,0:T(8,128)(2,1)} fusion(bf16[512,1024]{0,1:T(8,128)(2,1)S(1)} %bitcast.69, bf16[1024,1024]{1,0:T(8,128)(2,1)} %all-gather.5.cloned.1.call-done), kind=kOutput, calls=%fused_computation.35 | convolution fusion | flops 1074266112 | bytes 4194304 | tf_op jit(solution)/shard_map/dot_general | solution.py:93
  (114 shorter events, 55.0 us)
Async XLA Ops:
  7.2 39.3 %copy-start = (bf16[100,1024]{1,0:T(8,128)(2,1)S(1)}, bf16[100,1024]{1,0:T(8,128)(2,1)}, u32[]{:S(2)}) copy-start(bf16[100,1024]{1,0:T(8,128)(2,1)} %param.12) | copy-start | bytes 614404
  7.2 10.7 %copy-start.8 = (s32[32,128]{1,0:T(8,128)S(1)}, s32[32,128]{1,0:T(8,128)}, u32[]{:S(2)}) copy-start(s32[32,128]{1,0:T(8,128)} %param.10) | copy-start | bytes 49156
  7.2 121.0 %all-gather.3.cloned.1.call-start = ((), (), s32[]{:S(2)}) async-start(), calls=%async_computation | async-start | bytes 6684672 | tf_op jit(solution)/shard_map/all_gather | solution.py:33
  7.9 231.4 %all-gather.5.cloned.1.call-start = ((), (), s32[]{:S(2)}) async-start(), calls=%async_computation.1 | async-start | bytes 2228224 | tf_op jit(solution)/shard_map/all_gather | solution.py:34
  9.6 10.8 %collective-permute-start.1 = (bf16[100,1024]{0,1:T(8,128)(2,1)S(1)}, bf16[100,1024]{0,1:T(8,128)(2,1)S(1)}, u32[]{:S(2)}, u32[]{:S(2)}) collective-permute-start(bf16[100,1024]{0,1:T(8,128)(2,1)S(1)} %get-tuple-element.101), channel_id=1, source_target_pairs={{1,0},{2,1},{3,2},{4,3},{5,4},{6,5},{7,6},{8,7},{9,8},{10,9},{11,1... | collective-permute-start | bytes 614408 | tf_op jit(solution)/shard_map/ppermute | solution.py:18
  15.9 16.8 %collective-permute-start = (bf16[100,1024]{0,1:T(8,128)(2,1)S(1)}, bf16[100,1024]{0,1:T(8,128)(2,1)S(1)}, u32[]{:S(2)}, u32[]{:S(2)}) collective-permute-start(bf16[100,1024]{0,1:T(8,128)(2,1)S(1)} %get-tuple-element.100), channel_id=1, source_target_pairs={{0,1},{1,2},{2,3},{3,4},{4,5},{5,6},{6,7},{7,8},{8,9},{9,10},{10,1... | collective-permute-start | bytes 614408 | tf_op jit(solution)/shard_map/ppermute | solution.py:17
  33.0 12.8 %copy-start.11 = (bf16[32,16,128]{2,1,0:T(8,128)(2,1)S(1)}, bf16[32,16,128]{2,1,0:T(8,128)(2,1)}, u32[]{:S(2)}) copy-start(bf16[32,16,128]{2,1,0:T(8,128)(2,1)} %param.11) | copy-start | bytes 393220
  46.4 0.9 copy-start.9
  48.8 1.1 copy-start.5
  49.9 23.8 %collective-permute-start.3 = (bf16[256,1024]{1,0:T(8,128)(2,1)S(1)}, bf16[256,1024]{1,0:T(8,128)(2,1)S(1)}, u32[]{:S(2)}, u32[]{:S(2)}) collective-permute-start(bf16[256,1024]{1,0:T(8,128)(2,1)S(1)} %get-tuple-element.99), channel_id=1, source_target_pairs={{1,0},{2,1},{3,2},{4,3},{5,4},{6,5},{7,6},{8,7},{9,8},{10,9},{11,1... | collective-permute-start | bytes 1572872 | tf_op jit(solution)/shard_map/ppermute | solution.py:18
  51.8 30.7 %collective-permute-start.2 = (bf16[256,1024]{1,0:T(8,128)(2,1)S(1)}, bf16[256,1024]{1,0:T(8,128)(2,1)S(1)}, u32[]{:S(2)}, u32[]{:S(2)}) collective-permute-start(bf16[256,1024]{1,0:T(8,128)(2,1)S(1)} %get-tuple-element.98), channel_id=1, source_target_pairs={{0,1},{1,2},{2,3},{3,4},{4,5},{5,6},{6,7},{7,8},{8,9},{9,10},{10,1... | collective-permute-start | bytes 1572872 | tf_op jit(solution)/shard_map/ppermute | solution.py:17
  128.2 6.9 %copy-start.10 = (bf16[1024,3072]{1,0:T(8,128)(2,1)S(1)}, bf16[1024,3072]{1,0:T(8,128)(2,1)}, u32[]{:S(2)}) copy-start(bf16[1024,3072]{1,0:T(8,128)(2,1)} %all-gather.3.cloned.1.call-done) | copy-start | bytes 18874372
  132.9 2.0 copy-start.3
  134.9 1.2 copy-start.6
  139.5 3.0 %copy-start.2 = (f32[512,3072]{1,0:T(8,128)}, f32[512,3072]{1,0:T(8,128)S(1)}, u32[]{:S(2)}) copy-start(f32[512,3072]{1,0:T(8,128)S(1)} %fusion.24) | copy-start | bytes 18874372
  176.5 1.2 copy-start.4
  197.8 6.5 %copy-start.7 = (bf16[8,512,128]{1,2,0:T(8,128)(2,1)S(1)}, bf16[8,512,128]{1,2,0:T(8,128)(2,1)}, u32[]{:S(2)}) copy-start(bf16[8,512,128]{1,2,0:T(8,128)(2,1)} %custom-call.2) | copy-start | bytes 3145732
  239.3 3.9 %copy-start.1 = (bf16[100,1024]{1,0:T(8,128)(2,1)S(1)}, bf16[100,1024]{1,0:T(8,128)(2,1)}, u32[]{:S(2)}) copy-start(bf16[100,1024]{1,0:T(8,128)(2,1)} %param.12) | copy-start | bytes 614404
Sparse Core Ops, SparseCore 0:
  10.1 118.0 all-gather.2
  130.3 82.7 all-gather.4
where the time goes:
time: 251 us; the launch traced here: 250 us
  waiting for transfers between devices  89.3 us (36%)
  local copies, waits for them, and re-layouts  62.7 us (25%)
  other arithmetic  37.6 us (15%)
  matrix products  27.6 us (11%)
  between operations  14.3 us (6%)
  starting transfers between devices  12.8 us (5%)
  loops' own time  5.75 us (2%)
    all_gather x1, waiting for transfers between devices, shards(): lax.all_gather(w_qkv, 'dp', axis=0, tiled=True)  45.7 us
    ppermute x2, waiting for transfers between devices, padded(): after = lax.ppermute(first, axis, down)  21.8 us
    ppermute x2, waiting for transfers between devices, padded(): before = lax.ppermute(last, axis, up)  21.1 us
    concatenate x1, other arithmetic, shards(): jnp.concatenate([side_pairs[:margin], own_pairs, side_pairs[margin:]], ax...  20.1 us
    gather x2, local copies, waits for them, and re-layouts, shards(): picked = jnp.take(extended, cell_index, axis=1)  12.8 us
    div x6, local copies, waits for them, and re-layouts, unit_heads(): head_rows / scale_rows  11.2 us
    dynamic_slice x8, local copies, waits for them, and re-layouts, attend(): lax.dynamic_slice_in_dim(window, offset, group_width, 1)  8.56 us
    unnamed x25, local copies, waits for them, and re-layouts  8.42 us
  transfers between devices with their start and end apart: 6, of which 5 were waited for; matrix products, arithmetic and copies ran while one was open for 47% of the time, Pallas kernels for 0%

commit v1 on v0

--- a/solution.py
+++ b/solution.py
@@ -30,7 +30,9 @@
 def shards(fields, cell_index, interp_weight, w_in, ln_gain, w_qkv, w_out):
     width = w_qkv.shape[1] // 3
     full_qkv, full_out = (
-        lax.all_gather(w_qkv, "dp", axis=0, tiled=True),
+        jnp.concatenate(
+            lax.all_to_all(jnp.stack([w_qkv] * lax.axis_size("dp")), "dp", 0, 0), axis=0
+        ),
         lax.all_gather(w_out, "dp", axis=0, tiled=True),
     )
     grid_field = fields[0]

time: 251 us -> 329 us (1.31)
  the two profiles are of different devices: /device:TPU:256 before, /device:TPU:460 now
where the time goes in v1:
time: 329 us; the launch traced here: 328 us
  waiting for transfers between devices  143 us (43%)
  local copies, waits for them, and re-layouts  73.2 us (22%)
  other arithmetic  40.2 us (12%)
  matrix products  29.6 us (9%)
  starting transfers between devices  22 us (7%)
  between operations  14.3 us (4%)
  loops' own time  5.72 us (2%)
    ppermute x2, waiting for transfers between devices, padded(): after = lax.ppermute(first, axis, down)  108 us
    all_to_all x1, waiting for transfers between devices, shards(): lax.all_to_all(jnp.stack([w_qkv] * lax.axis_size('dp')), 'dp', 0, 0)  29.1 us
    concatenate x1, other arithmetic, shards(): jnp.concatenate([side_pairs[:margin], own_pairs, side_pairs[margin:]], ax...  20.4 us
    div x6, local copies, waits for them, and re-layouts, unit_heads(): head_rows / scale_rows  13.6 us
    gather x2, local copies, waits for them, and re-layouts, shards(): picked = jnp.take(extended, cell_index, axis=1)  12.8 us
    ppermute x2, starting transfers between devices, padded(): after = lax.ppermute(first, axis, down)  10.1 us
    mul x3, local copies, waits for them, and re-layouts, unit_heads(): head_rows * head_rows  8.77 us
    dynamic_slice x8, local copies, waits for them, and re-layouts, attend(): lax.dynamic_slice_in_dim(window, offset, group_width, 1)  8.56 us
  transfers between devices with their start and end apart: 6, of which 5 were waited for; matrix products, arithmetic and copies ran while one was open for 40% of the time, Pallas kernels for 0%

profile of v1, /device:TPU:460, one launch (start us, length us, event | category | flops | bytes accessed | tf_op | source)
XLA Modules:
  0.0 328.1 jit_solution(5546577344834277139)
XLA Ops:
  7.2 4.5 %stack.2 = bf16[16,64,3072]{2,1,0:T(8,128)(2,1)} broadcast(bf16[64,3072]{1,0:T(8,128)(2,1)} %param.14), dimensions={1,2} | broadcast | bytes 6684672 | tf_op jit(solution)/shard_map/stack | solution.py:34
  11.7 7.9 %all-to-all-start = ((bf16[16,64,3072]{2,1,0:T(8,128)(2,1)}), bf16[16,64,3072]{2,1,0:T(8,128)(2,1)}, u32[]{:S(2)}, u32[]{:S(2)}) async-start(bf16[16,64,3072]{2,1,0:T(8,128)(2,1)} %stack.2), calls=%async_computation | async-start | bytes 12582912 | tf_op jit(solution)/shard_map/all_to_all | solution.py:34
  20.3 3.9 %collective-permute-start.1 = (bf16[100,1024]{0,1:T(8,128)(2,1)S(1)}, bf16[100,1024]{0,1:T(8,128)(2,1)S(1)}, u32[]{:S(2)}, u32[]{:S(2)}) collective-permute-start(bf16[100,1024]{0,1:T(8,128)(2,1)S(1)} %get-tuple-element.101), channel_id=1, source_target_pairs={{1,0},{2,1},{3,2},{4,3},{5,4},{6,5},{7,6},{8,7},{9,8},{10,9},{11,1... | collective-permute-start | bytes 614408 | tf_op jit(solution)/shard_map/ppermute | solution.py:18
  26.2 74.8 %collective-permute-done.1 = bf16[100,1024]{0,1:T(8,128)(2,1)S(1)} collective-permute-done((bf16[100,1024]{0,1:T(8,128)(2,1)S(1)}, bf16[100,1024]{0,1:T(8,128)(2,1)S(1)}, u32[]{:S(2)}, u32[]{:S(2)}) %collective-permute-start.1) | collective-permute-done | bytes 204832 | tf_op jit(solution)/shard_map/ppermute | solution.py:18
  101.0 2.6 collective-permute-done
  103.9 12.1 %gather_fusion = bf16[4096,100]{1,0:T(8,128)(2,1)S(1)} fusion(bf16[100,6144]{0,1:T(8,128)(2,1)S(1)} %pad_maximum_fusion, s32[4096]{0:T(1024)S(1)} %bitcast_clamp_fusion), kind=kCustom, calls=%fused_computation | custom fusion | bytes 1654784 | tf_op jit(solution)/shard_map/jit(_take)/gather | solution.py:42
  119.7 6.2 %collective-permute-start.3 = (bf16[256,1024]{1,0:T(8,128)(2,1)S(1)}, bf16[256,1024]{1,0:T(8,128)(2,1)S(1)}, u32[]{:S(2)}, u32[]{:S(2)}) collective-permute-start(bf16[256,1024]{1,0:T(8,128)(2,1)S(1)} %get-tuple-element.99), channel_id=1, source_target_pairs={{1,0},{2,1},{3,2},{4,3},{5,4},{6,5},{7,6},{8,7},{9,8},{10,9},{11,1... | collective-permute-start | bytes 1572872 | tf_op jit(solution)/shard_map/ppermute | solution.py:18
  128.0 32.7 %collective-permute-done.3 = bf16[256,1024]{1,0:T(8,128)(2,1)S(1)} collective-permute-done((bf16[256,1024]{1,0:T(8,128)(2,1)S(1)}, bf16[256,1024]{1,0:T(8,128)(2,1)S(1)}, u32[]{:S(2)}, u32[]{:S(2)}) %collective-permute-start.3) | collective-permute-done | bytes 524320 | tf_op jit(solution)/shard_map/ppermute | solution.py:18
  160.7 3.8 %collective-permute-done.2 = bf16[256,1024]{1,0:T(8,128)(2,1)S(1)} collective-permute-done((bf16[256,1024]{1,0:T(8,128)(2,1)S(1)}, bf16[256,1024]{1,0:T(8,128)(2,1)S(1)}, u32[]{:S(2)}, u32[]{:S(2)}) %collective-permute-start.2) | collective-permute-done | bytes 524320 | tf_op jit(solution)/shard_map/ppermute | solution.py:17
  164.6 29.1 %all-to-all-done = bf16[16,64,3072]{2,1,0:T(8,128)(2,1)} async-done(((bf16[16,64,3072]{2,1,0:T(8,128)(2,1)}), bf16[16,64,3072]{2,1,0:T(8,128)(2,1)}, u32[]{:S(2)}, u32[]{:S(2)}) %all-to-all-start) | async-done | bytes 6291488 | tf_op jit(solution)/shard_map/all_to_all | solution.py:34
  193.6 4.5 %fusion.8 = f32[512,2048]{1,0:T(8,128)S(1)} fusion(bf16[1024,3072]{1,0:T(8,128)(2,1)} %bitcast.13, bf16[256,1024]{1,0:T(8,128)(2,1)S(1)} %collective-permute-done.3, bf16[256,1024]{1,0:T(8,128)(2,1)S(1)} %collective-permute-done.2), kind=kOutput, calls=%fused_computation.16 | convolution fusion | flops 2149580800 | bytes 9437184 | tf_op jit(solution)/shard_map/dot_general | solution.py:55
  201.8 5.5 %fusion.24 = f32[512,3072]{1,0:T(8,128)S(1)} fusion(bf16[512,1024]{1,0:T(8,128)(2,1)S(1)} %get-tuple-element.96, bf16[1024,3072]{1,0:T(8,128)(2,1)} %bitcast.13), kind=kOutput, calls=%fused_computation.59 | convolution fusion | flops 3221225472 | bytes 13631488 | tf_op jit(solution)/shard_map/dot_general | solution.py:54
  212.4 2.9 copy.15
  218.8 2.9 copy.16
  221.7 2.6 divide_convert_fusion.6
  224.4 2.9 copy.19
  230.8 2.9 copy.20
  233.7 2.9 copy.17
  240.2 2.9 copy.18
  243.1 5.3 %divide_convert_fusion.4 = (bf16[512,1024]{1,0:T(8,128)(2,1)}, bf16[512,1024]{1,0:T(8,128)(2,1)S(1)}) fusion(f32[512,1024]{1,0:T(8,128)} %copy.20, f32[512,3072]{1,0:T(8,128)} %copy-done.2, f32[512,1024]{1,0:T(8,128)} %copy.18), kind=kLoop, calls=%fused_computation.25 | loop fusion | flops 2097152 | bytes 10485760 | tf_op jit(solution)/shard_map/convert_element_type | solution.py:27
  248.5 20.4 %fusion.7 = bf16[1024,2048]{1,0:T(8,128)(2,1)} fusion(bf16[512,1024]{1,0:T(8,128)(2,1)S(1)} %slice.81, bf16[512,1024]{1,0:T(8,128)(2,1)S(1)} %divide_convert_fusion.6, bf16[512,1024]{1,0:T(8,128)(2,1)S(1)} %slice.80, bf16[512,1024]{1,0:T(8,128)(2,1)S(1)} %get-tuple-element.93, bf16[256,2048]{1,0:T(8,128)(2,1)S(1)} %fusion.11), kind=kLoop, calls=%fused_computation.15 | loop fusion | flops 27262976 | bytes 9437184 | tf_op jit(solution)/shard_map/concatenate | solution.py:68
  268.9 6.5 %copy.21 = bf16[1024,2048]{0,1:T(8,128)(2,1)} copy(bf16[1024,2048]{1,0:T(8,128)(2,1)} %fusion.7) | data formatting | bytes 8388608 | tf_op jit(solution)/shard_map/while | solution.py:93
  275.4 41.9 %while.12 = (s32[]{:T(128)}, bf16[8,512,128]{1,2,0:T(8,128)(2,1)S(1)}, s32[8]{0:T(128)S(1)}, bf16[1024,2048]{0,1:T(8,128)(2,1)}, bf16[512,1024]{1,0:T(8,128)(2,1...) while((s32[]{:T(128)}, ...), condition=%wide.region_7.8_spmd, body=%wide.region_5.7_spmd.sunk | while | flops 273742848 | bytes 11018490 | solution.py:93
  317.4 3.9 %fusion.10 = bf16[1,512,1024]{2,1,0:T(8,128)(2,1)} fusion(bf16[512,1024]{0,1:T(8,128)(2,1)S(1)} %bitcast.70, bf16[1024,1024]{1,0:T(8,128)(2,1)} %all-gather.2.cloned.1.call-done), kind=kOutput, calls=%fused_computation.35 | convolution fusion | flops 1074266112 | bytes 4194304 | tf_op jit(solution)/shard_map/dot_general | solution.py:95
  (108 shorter events, 64.2 us)
Async XLA Ops:
  7.2 110.1 %copy-start = (bf16[100,1024]{1,0:T(8,128)(2,1)S(1)}, bf16[100,1024]{1,0:T(8,128)(2,1)}, u32[]{:S(2)}) copy-start(bf16[100,1024]{1,0:T(8,128)(2,1)} %param.12) | copy-start | bytes 614404
  11.7 7.9 %copy-start.5 = (bf16[1,100,4096]{2,1,0:T(8,128)(2,1)S(1)}, bf16[1,100,4096]{2,1,0:T(8,128)(2,1)}, u32[]{:S(2)}) copy-start(bf16[1,100,4096]{2,1,0:T(8,128)(2,1)} %param.9) | copy-start | bytes 2457604
  11.7 182.0 %all-to-all-start = ((bf16[16,64,3072]{2,1,0:T(8,128)(2,1)}), bf16[16,64,3072]{2,1,0:T(8,128)(2,1)}, u32[]{:S(2)}, u32[]{:S(2)}) async-start(bf16[16,64,3072]{2,1,0:T(8,128)(2,1)} %stack.2), calls=%async_computation | async-start | bytes 12582912 | tf_op jit(solution)/shard_map/all_to_all | solution.py:34
  19.5 6.7 %copy-start.6 = (s32[32,128]{1,0:T(8,128)S(1)}, s32[32,128]{1,0:T(8,128)}, u32[]{:S(2)}) copy-start(s32[32,128]{1,0:T(8,128)} %param.10) | copy-start | bytes 49156
  19.5 297.8 %all-gather.2.cloned.1.call-start = ((), (), s32[]{:S(2)}) async-start(), calls=%async_computation.1 | async-start | bytes 2228224 | tf_op jit(solution)/shard_map/all_gather | solution.py:36
  20.3 80.7 %collective-permute-start.1 = (bf16[100,1024]{0,1:T(8,128)(2,1)S(1)}, bf16[100,1024]{0,1:T(8,128)(2,1)S(1)}, u32[]{:S(2)}, u32[]{:S(2)}) collective-permute-start(bf16[100,1024]{0,1:T(8,128)(2,1)S(1)} %get-tuple-element.101), channel_id=1, source_target_pairs={{1,0},{2,1},{3,2},{4,3},{5,4},{6,5},{7,6},{8,7},{9,8},{10,9},{11,1... | collective-permute-start | bytes 614408 | tf_op jit(solution)/shard_map/ppermute | solution.py:18
  24.3 79.3 %collective-permute-start = (bf16[100,1024]{0,1:T(8,128)(2,1)S(1)}, bf16[100,1024]{0,1:T(8,128)(2,1)S(1)}, u32[]{:S(2)}, u32[]{:S(2)}) collective-permute-start(bf16[100,1024]{0,1:T(8,128)(2,1)S(1)} %get-tuple-element.100), channel_id=1, source_target_pairs={{0,1},{1,2},{2,3},{3,4},{4,5},{5,6},{6,7},{7,8},{8,9},{9,10},{10,1... | collective-permute-start | bytes 614408 | tf_op jit(solution)/shard_map/ppermute | solution.py:17
  103.9 12.8 %copy-start.8 = (bf16[32,16,128]{2,1,0:T(8,128)(2,1)S(1)}, bf16[32,16,128]{2,1,0:T(8,128)(2,1)}, u32[]{:S(2)}) copy-start(bf16[32,16,128]{2,1,0:T(8,128)(2,1)} %param.11) | copy-start | bytes 393220
  117.3 0.9 copy-start.7
  119.7 41.0 %collective-permute-start.3 = (bf16[256,1024]{1,0:T(8,128)(2,1)S(1)}, bf16[256,1024]{1,0:T(8,128)(2,1)S(1)}, u32[]{:S(2)}, u32[]{:S(2)}) collective-permute-start(bf16[256,1024]{1,0:T(8,128)(2,1)S(1)} %get-tuple-element.99), channel_id=1, source_target_pairs={{1,0},{2,1},{3,2},{4,3},{5,4},{6,5},{7,6},{8,7},{9,8},{10,9},{11,1... | collective-permute-start | bytes 1572872 | tf_op jit(solution)/shard_map/ppermute | solution.py:18
  125.9 38.7 %collective-permute-start.2 = (bf16[256,1024]{1,0:T(8,128)(2,1)S(1)}, bf16[256,1024]{1,0:T(8,128)(2,1)S(1)}, u32[]{:S(2)}, u32[]{:S(2)}) collective-permute-start(bf16[256,1024]{1,0:T(8,128)(2,1)S(1)} %get-tuple-element.98), channel_id=1, source_target_pairs={{0,1},{1,2},{2,3},{3,4},{4,5},{5,6},{6,7},{7,8},{8,9},{9,10},{10,1... | collective-permute-start | bytes 1572872 | tf_op jit(solution)/shard_map/ppermute | solution.py:17
  198.2 2.0 copy-start.3
  207.3 2.7 copy-start.2
  268.9 6.5 %copy-start.4 = (bf16[8,512,128]{1,2,0:T(8,128)(2,1)S(1)}, bf16[8,512,128]{1,2,0:T(8,128)(2,1)}, u32[]{:S(2)}) copy-start(bf16[8,512,128]{1,2,0:T(8,128)(2,1)} %custom-call.2) | copy-start | bytes 3145732
  317.3 3.9 %copy-start.1 = (bf16[100,1024]{1,0:T(8,128)(2,1)S(1)}, bf16[100,1024]{1,0:T(8,128)(2,1)}, u32[]{:S(2)}) copy-start(bf16[100,1024]{1,0:T(8,128)(2,1)} %param.12) | copy-start | bytes 614404
Sparse Core Ops, SparseCore 0:
  128.1 121.1 all-gather.1
